TPU v7x, 512 devices: a whole 4x4x16 slice. The times are simulated.
512 devices in a mesh: seq: 64 (over x, z), tensor: 8 (over y, core).
Axes of the slice: x: 4, y: 4, z: 16, core: 2. Of those that a mesh axis runs over, the one named last changes fastest.
Arguments:
- hidden: bfloat16 [8, 16384, 8192], P(None, 'seq', 'tensor'), may hold values from -160 to 160
- norm_gain: bfloat16 [8192], P('tensor'), may hold values from 0.25 to 1.75
- value_weight: bfloat16 [8192], P('tensor'), may hold values from -0.0625 to 0.0625
- rewards: float32 [8, 16384], P(None, 'seq'), may hold values from -6 to 6
- done_flags: int32 [8, 16384], P(None, 'seq'), may hold values 0 or 1
- valid_mask: int32 [8, 16384], P('tensor', 'seq'), may hold values 0 or 1
- new_logprob: float32 [8, 16384], P('tensor', 'seq'), may hold values from -1 to 1
- old_logprob: float32 [8, 16384], P('tensor', 'seq'), may hold values from -1 to 1
- discount: float32 [8], replicated, may hold values from 0.9 to 1
- trace_decay: float32 [8], replicated, may hold values from 0.9 to 1
- bootstrap: float32 [8], replicated, may hold values from -5 to 5
Outputs:
- values: float32 [8, 16384], P('tensor', 'seq')
- white_adv: float32 [8, 16384], P('tensor', 'seq')
- token_loss: float32 [8, 16384], P('tensor', 'seq')
- policy_loss: float32 [], replicated
All inputs are finite; a program needn't handle non-finite values. No bound on the sum of `done_flags` or of `valid_mask` on one device may be relied on, other than what follows from the above.
Results may differ from a plain program's by a relative error of at most 0.00035.
Values sent between devices are 32-bit elements; how exact they have to be, the bound alone decides.
A program may use at most 64 MiB of HBM per device.

v0:
```python
import jax
import jax.numpy as jnp
from jax import lax
from jax.sharding import Mesh
from jax.sharding import PartitionSpec as P

H = 8192
TENSOR = ("tensor_0", "tensor_1")
SEQ = ("seq_0", "seq_1")


EPS_NORM = 1e-06
EPS_WHITE = 1e-08
CLIP = 0.2
HIGHEST = lax.Precision.HIGHEST


def from_everyone(x, axis):
    devices = lax.axis_size(axis)
    return lax.all_to_all(jnp.broadcast_to(x[None], (devices, *x.shape)), axis, 0, 0, tiled=True)


def of_everyone(x, axis):
    everything = from_everyone(x, axis)
    return jnp.sum(everything, axis=0)


def packed_total(arrays, axis):
    vector, at, gathered = (jnp.concatenate([a.reshape(-1) for a in arrays]), 0, [])
    so_far = of_everyone(vector, axis)
    for a in arrays:
        gathered.append(so_far[at : at + a.size].reshape(a.shape))
        at += a.size
    return tuple(gathered)


def joined_along(tiles, dim):
    tiles = jnp.moveaxis(tiles, 0, dim)
    lengths = tiles.shape
    return tiles.reshape(*lengths[:dim], lengths[dim] * lengths[dim + 1], *lengths[dim + 2 :])


def gather_axes(x, axes, dim):
    far, near = axes
    tiles = from_everyone(from_everyone(x, far), near)
    return joined_along(tiles.swapaxes(0, 1).reshape(-1, *x.shape), dim)


def one_axis_at_a_time(x, axes):
    far, near = axes
    return of_everyone(of_everyone(x, near), far)


def compose(earlier, later):
    return (later[0] + later[1] * earlier[0], later[1] * earlier[1])


def local_pass(values, rewards, done_flags, discount, trace_decay):
    row_count, length = values.shape
    alive = 1.0 - done_flags.astype(jnp.float32)
    inner_next = jnp.concatenate([values[:, 1:], jnp.zeros((row_count, 1), jnp.float32)], axis=1)
    delta = rewards + discount[:, None] * alive * inner_next - values
    decay = discount * trace_decay
    counted = jnp.cumsum(done_flags, axis=1) - done_flags
    later_pos = lax.broadcasted_iota(jnp.int32, (length, length), 1)
    early_pos = lax.broadcasted_iota(jnp.int32, (length, length), 0)
    upper = later_pos >= early_pos
    distance = jnp.maximum(later_pos - early_pos, 0).astype(jnp.float32)
    powers = jnp.exp(distance[None, :, :] * jnp.log(decay)[:, None, None])
    same_episode = counted[:, None, :] == counted[:, :, None]
    weights = jnp.where(upper[None, :, :] & same_episode, powers, 0.0)
    local_adv = jnp.einsum(
        "stj,sj->st", weights, delta, precision=HIGHEST, preferred_element_type=jnp.float32
    )
    coef = weights[:, :, length - 1] * (discount * alive[:, length - 1])[:, None]
    return (local_adv, coef)


def fold_step(carry, block):
    return (compose(carry, block), carry)


def shards(
    hidden,
    norm_gain,
    value_weight,
    rewards,
    done_flags,
    valid_mask,
    new_logprob,
    old_logprob,
    discount,
    trace_decay,
    bootstrap,
):
    seqs_all = hidden.shape[0]
    own_rows = seqs_all // lax.axis_size(TENSOR)
    first_row = lax.axis_index(TENSOR) * own_rows
    scaled = norm_gain.astype(jnp.float32) * value_weight.astype(jnp.float32)
    squares = jnp.einsum("sth,sth->st", hidden, hidden, preferred_element_type=jnp.float32)
    products = jnp.einsum(
        "sth,h->st", hidden, scaled, precision=HIGHEST, preferred_element_type=jnp.float32
    )
    squares, products = packed_total((squares, products), TENSOR)
    values = products * lax.rsqrt(squares / H + EPS_NORM)
    local_adv, coef = local_pass(values, rewards, done_flags, discount, trace_decay)
    values_own = lax.dynamic_slice_in_dim(values, first_row, own_rows, 0)
    weight = valid_mask.astype(jnp.float32)
    offset = values[:, 0] + trace_decay * local_adv[:, 0]
    slope = trace_decay * coef[:, 0]
    local_own = lax.dynamic_slice_in_dim(local_adv, first_row, own_rows, 0)
    coef_own = lax.dynamic_slice_in_dim(coef, first_row, own_rows, 0)
    offset_own = lax.dynamic_slice_in_dim(offset, first_row, own_rows, 0)
    slope_own = lax.dynamic_slice_in_dim(slope, first_row, own_rows, 0)
    packed = jnp.stack(
        [
            offset_own,
            slope_own,
            jnp.sum(weight, axis=1),
            jnp.sum(weight * local_own, axis=1),
            jnp.sum(weight * coef_own, axis=1),
            jnp.sum(weight * local_own * local_own, axis=1),
            jnp.sum(weight * local_own * coef_own, axis=1),
            jnp.sum(weight * coef_own * coef_own, axis=1),
        ],
        axis=1,
    )
    gathered = gather_axes(packed[None], (("seq_0", "seq_1"), ("tensor_0", "tensor_1")), 0)
    seq_count = lax.axis_size(SEQ)
    table = gathered.reshape(seq_count, seqs_all, 8)
    start_pair = (jnp.zeros((seqs_all,), jnp.float32), jnp.ones((seqs_all,), jnp.float32))
    _, prefix = lax.scan(fold_step, start_pair, (table[:, :, 0], table[:, :, 1]), reverse=True)
    entering = prefix[0] + prefix[1] * bootstrap[None, :]
    count = jnp.sum(table[:, :, 2])
    total = jnp.sum(table[:, :, 3] + entering * table[:, :, 4])
    square_sum = jnp.sum(
        table[:, :, 5] + 2.0 * entering * table[:, :, 6] + entering * entering * table[:, :, 7]
    )
    mean = total / count
    variance = square_sum / count - mean * mean
    own_entering = lax.dynamic_slice_in_dim(
        lax.dynamic_index_in_dim(entering, lax.axis_index(SEQ), 0, False), first_row, own_rows, 0
    )
    adv_own = local_own + coef_own * own_entering[:, None]
    white_adv = (adv_own - mean) * lax.rsqrt(variance + EPS_WHITE)
    ratio = jnp.exp(new_logprob - old_logprob)
    surrogate = jnp.minimum(ratio * white_adv, jnp.clip(ratio, 1.0 - CLIP, 1.0 + CLIP) * white_adv)
    token_loss = -weight * surrogate
    loss_sum = one_axis_at_a_time(
        jnp.sum(token_loss), (("seq_0", "seq_1"), ("tensor_0", "tensor_1"))
    )
    policy_loss = loss_sum / count
    return (values_own, white_adv, token_loss, policy_loss)


def solution(mesh):
    split = Mesh(mesh.devices.reshape(4, 16, 4, 2), ("seq_0", "seq_1", "tensor_0", "tensor_1"))
    in_specs = (
        P(None, SEQ, TENSOR),
        P(TENSOR),
        P(TENSOR),
        P(None, SEQ),
        P(None, SEQ),
        P(TENSOR, SEQ),
        P(TENSOR, SEQ),
        P(TENSOR, SEQ),
        P(),
        P(),
        P(),
    )
    out_specs = (P(TENSOR, SEQ), P(TENSOR, SEQ), P(TENSOR, SEQ), P())
    return jax.shard_map(
        shards, mesh=split, in_specs=in_specs, out_specs=out_specs, check_vma=False
    )
```

profile of v0, /device:TPU:1, one launch (start us, length us, event | category | flops | bytes accessed | tf_op | source)
XLA Modules:
  0.0 119.2 jit_solution(13456207747296009241)
XLA Ops:
  0.7 3.2 %fusion.3 = f32[8,256]{1,0:T(8,128)S(1)} fusion(bf16[8,256,1024]{2,1,0:T(8,128)(2,1)} %param.13), kind=kLoop, calls=%fused_computation.9 | loop fusion | flops 6289408 | bytes 4202496 | tf_op jit(solution)/shard_map/sth,sth->st/dot_general | solution.py:100
  3.9 0.2 copy-done
  4.1 3.3 %fusion.15 = f32[1,8,256]{2,0,1:T(1,128)S(1)} fusion(f32[1024,1,1]{0,1,2:T(1,128)S(1)} %bitcast.78, bf16[8,256,1024]{2,1,0:T(8,128)(2,1)S(1)} %copy-done), kind=kOutput, calls=%fused_computation.57 | convolution fusion | flops 25165824 | bytes 4206592 | tf_op jit(solution)/shard_map/sth,h->st/dot_general | solution.py:101
  7.5 0.7 broadcast_in_dim.65
  8.2 10.1 %all-to-all-start = ((f32[8,1,4096]{2,1,0:T(1,128)}), f32[8,1,4096]{2,1,0:T(1,128)S(1)}, u32[]{:S(2)}, u32[]{:S(2)}) async-start(f32[8,1,4096]{2,1,0:T(1,128)} %broadcast_in_dim.65), calls=%async_computation | async-start | bytes 262144 | tf_op jit(solution)/shard_map/all_to_all | solution.py:20
  18.3 0.6 reduce-window.6
  18.9 0.2 slice_reduce_fusion
  19.2 0.1 bitcast_subtract_fusion
  19.3 0.1 copy.38
  19.5 4.1 %all-to-all-done = f32[8,1,4096]{2,1,0:T(1,128)S(1)} async-done(((f32[8,1,4096]{2,1,0:T(1,128)}), f32[8,1,4096]{2,1,0:T(1,128)S(1)}, u32[]{:S(2)}, u32[]{:S(2)}) %all-to-all-start) | async-done | bytes 131104 | tf_op jit(solution)/shard_map/all_to_all | solution.py:20
  23.6 0.1 reduce_sum.117
  23.7 0.1 slice.91
  23.8 0.1 slice_reduce_fusion.4
  23.9 0.1 convert_subtract_fusion
  24.0 0.2 slice_reduce_fusion.5
  24.2 0.7 exponential_select_fusion
  25.0 0.1 fusion.6
  25.0 1.7 %fusion.4 = f32[8,1,256]{2,1,0:T(1,128)S(1)} fusion(f32[8,256,256]{1,0,2:T(8,128)S(1)} %exponential_select_fusion, f32[8,256,1]{1,0,2:T(8,128)S(1)} %get-tuple-element.232), kind=kOutput, calls=%fused_computation.10 | convolution fusion | flops 6291456 | bytes 2113536 | tf_op jit(solution)/shard_map/stj,sj->st/dot_general | solution.py:72
  26.8 0.1 slice_reduce_fusion.2
  26.9 0.6 dynamic_slice.43
  27.5 0.6 dynamic_slice.42
  28.1 0.7 multiply_reduce_fusion
  28.8 5.2 %stack.35 = f32[1,8]{1,0:T(1,128)S(1)} concatenate(f32[1,1]{1,0:T(1,128)} %bitcast.7, f32[1,1]{1,0:T(1,128)} %bitcast.8, f32[1,1]{1,0:T(1,128)} %bitcast.9, f32[1,1]{1,0:T(1,128)} %bitcast.10, f32[1,1]{1,0:T(1,128)} %bitcast.11, f32[1,1]{1,0:T(1,128)} %bitcast.12, f32[1,1]{1,0:T(1,128)} %bitcast.13, f32[1,1]{1,0:T(1,128)} %bitcast.14), dimensions={1} | concatenate | bytes 64 | tf_op jit(solution)/shard_map/stack | solution.py:115
  34.0 27.2 %all_to_all.28 = f32[64,1,1,8]{3,2,1,0:T(1,128)S(1)} all-to-all(f32[64,1,1,8]{3,2,1,0:T(1,128)S(1)} %broadcast_in_dim.68), channel_id=1, replica_groups=mesh['seq_0'=4,'seq_1'=16,'tensor_0'=4,'tensor_1'=2] {'seq_0','seq_1'}, dimensions={0} | all-to-all | bytes 4096 | tf_op jit(solution)/shard_map/all_to_all | solution.py:20
  61.3 0.1 copy.39
  61.3 0.7 reshape.119
  62.0 5.5 %all-to-all-start.2 = ((f32[8,1,512]{2,1,0:T(1,128)}), f32[8,1,512]{2,1,0:T(1,128)S(1)}, u32[]{:S(2)}, u32[]{:S(2)}) async-start(f32[8,1,512]{2,1,0:T(1,128)} %reshape.119), calls=%async_computation.2 | async-start | bytes 32768 | tf_op jit(solution)/shard_map/all_to_all | solution.py:20
  67.5 4.7 %all-to-all-done.2 = f32[8,1,512]{2,1,0:T(1,128)S(1)} async-done(((f32[8,1,512]{2,1,0:T(1,128)}), f32[8,1,512]{2,1,0:T(1,128)S(1)}, u32[]{:S(2)}, u32[]{:S(2)}) %all-to-all-start.2) | async-done | bytes 16416 | tf_op jit(solution)/shard_map/all_to_all | solution.py:20
  72.2 0.5 broadcast.79
  72.7 0.7 reduce.22
  73.4 0.1 reshape.120
  73.5 0.6 slice_reduce_fusion.1
  74.1 0.1 copy.40
  74.2 0.1 copy.41
  74.3 7.4 %while.21 = (s32[]{:T(128)}, f32[8]{0:T(128)S(1)}, f32[8]{0:T(128)S(1)}, f32[64,8]{1,0:T(8,128)S(1)}, f32[64,8]{1,0:T(8,128)S(1)}, /*index=5*/f32[64,8]{1,0:T(8,...) while((s32[]{:T(128)}, f32[8]{0:T(128)S(1)}, f32[8]{0:T(128)S(1)}, ...), condition=%wide.region_10.11_spmd.clone, body=%wide.region_9.10_spmd.clone.sunk | while | flops 44 | bytes 519 | solution.py:132
  81.7 0.1 copy.42
  81.7 0.1 copy.43
  81.8 0.7 add_reduce_fusion.1
  85.2 0.6 dynamic_slice.44
  85.8 1.9 %fusion.12 = (f32[]{:T(128)}, f32[1,256]{1,0:T(1,128)}, f32[1,256]{1,0:T(1,128)}) fusion(f32[1,256]{1,0:T(1,128)S(1)} %copy-done.8, f32[1,256]{1,0:T(1,128)S(1)} %copy-done.9, s32[1,256]{1,0:T(1,128)S(1)} %copy-done.3, f32[]{:T(128)S(6)} %rsqrt.8, f32[]{:T(128)S(6)} %div.17, f32[]{:T(128)} %bitcast.22, f32[8,256]{1,0:T(8,128)S(1)} %fusion.6, ...), kind=kLoop, calls=%fused_computation.52 | loop fusion | flops 3327 | bytes 7188 | tf_op jit(solution)/shard_map/reduce_sum | solution.py:150
  87.7 0.7 broadcast_in_dim.71
  88.4 7.7 %all_to_all.29 = f32[8,1,1]{2,1,0:T(1,128)S(1)} all-to-all(f32[8,1,1]{2,1,0:T(1,128)S(1)} %broadcast_in_dim.71), channel_id=1, replica_groups=mesh['seq_0'=4,'seq_1'=16,'tensor_0'=4,'tensor_1'=2] {'tensor_0','tensor..., dimensions={0} | all-to-all | bytes 64 | tf_op jit(solution)/shard_map/all_to_all | solution.py:20
  96.1 0.6 reduce_sum.128
  96.7 1.3 %broadcast_in_dim.72 = f32[64,1,1]{2,1,0:T(1,128)} broadcast(f32[]{:T(128)} %reduce_sum.128), dimensions={} | broadcast | bytes 260 | tf_op jit(solution)/shard_map/broadcast_in_dim | solution.py:20
  98.0 4.6 %all-to-all-start.4 = ((f32[64,1,1]{2,1,0:T(1,128)}), f32[64,1,1]{2,1,0:T(1,128)S(1)}, u32[]{:S(2)}, u32[]{:S(2)}) async-start(f32[64,1,1]{2,1,0:T(1,128)} %broadcast_in_dim.72), calls=%async_computation.4 | async-start | bytes 65536 | tf_op jit(solution)/shard_map/all_to_all | solution.py:20
  102.6 0.6 constant_dynamic-slice_fusion.3
  103.1 12.8 %all-to-all-done.4 = f32[64,1,1]{2,1,0:T(1,128)S(1)} async-done(((f32[64,1,1]{2,1,0:T(1,128)}), f32[64,1,1]{2,1,0:T(1,128)S(1)}, u32[]{:S(2)}, u32[]{:S(2)}) %all-to-all-start.4) | async-done | bytes 288 | tf_op jit(solution)/shard_map/all_to_all | solution.py:20
  115.9 0.7 reduce_sum.129
  (234 shorter events, 6.3 us)
Async XLA Ops:
  0.6 3.5 %copy-start = (bf16[8,256,1024]{2,1,0:T(8,128)(2,1)S(1)}, bf16[8,256,1024]{2,1,0:T(8,128)(2,1)}, u32[]{:S(2)}) copy-start(bf16[8,256,1024]{2,1,0:T(8,128)(2,1)} %param.13) | copy-start | bytes 12582916
  0.6 3.2 %copy-start.7 = (bf16[1024]{0:T(1024)(128)(2,1)S(1)}, bf16[1024]{0:T(1024)(128)(2,1)}, u32[]{:S(2)}) copy-start(bf16[1024]{0:T(1024)(128)(2,1)} %param.14) | copy-start | bytes 6148
  0.7 3.2 %copy-start.6 = (bf16[1024]{0:T(1024)(128)(2,1)S(1)}, bf16[1024]{0:T(1024)(128)(2,1)}, u32[]{:S(2)}) copy-start(bf16[1024]{0:T(1024)(128)(2,1)} %param.15) | copy-start | bytes 6148
  4.1 14.2 %copy-start.1 = (s32[8,256]{1,0:T(8,128)S(1)}, s32[8,256]{1,0:T(8,128)}, u32[]{:S(2)}) copy-start(s32[8,256]{1,0:T(8,128)} %param.17) | copy-start | bytes 24580
  4.1 19.8 %copy-start.2 = (f32[8,256]{1,0:T(8,128)S(1)}, f32[8,256]{1,0:T(8,128)}, u32[]{:S(2)}) copy-start(f32[8,256]{1,0:T(8,128)} %param.16) | copy-start | bytes 24580
  4.1 19.8 %copy-start.4 = (f32[8]{0:T(128)S(1)}, f32[8]{0:T(128)}, u32[]{:S(2)}) copy-start(f32[8]{0:T(128)} %param.21) | copy-start | bytes 100
  4.1 20.1 %copy-start.5 = (f32[8]{0:T(128)S(1)}, f32[8]{0:T(128)}, u32[]{:S(2)}) copy-start(f32[8]{0:T(128)} %param.22) | copy-start | bytes 100
  8.2 15.4 %all-to-all-start = ((f32[8,1,4096]{2,1,0:T(1,128)}), f32[8,1,4096]{2,1,0:T(1,128)S(1)}, u32[]{:S(2)}, u32[]{:S(2)}) async-start(f32[8,1,4096]{2,1,0:T(1,128)} %broadcast_in_dim.65), calls=%async_computation | async-start | bytes 262144 | tf_op jit(solution)/shard_map/all_to_all | solution.py:20
  24.2 3.9 %copy-start.3 = (s32[1,256]{1,0:T(1,128)S(1)}, s32[1,256]{1,0:T(1,128)}, u32[]{:S(2)}) copy-start(s32[1,256]{1,0:T(1,128)} %param.18) | copy-start | bytes 3076
  24.9 56.9 %copy-start.10 = (f32[8]{0:T(128)S(1)}, f32[8]{0:T(128)}, u32[]{:S(2)}) copy-start(f32[8]{0:T(128)} %param.23) | copy-start | bytes 100
  24.9 60.9 %copy-start.8 = (f32[1,256]{1,0:T(1,128)S(1)}, f32[1,256]{1,0:T(1,128)}, u32[]{:S(2)}) copy-start(f32[1,256]{1,0:T(1,128)} %param.19) | copy-start | bytes 3076
  25.0 60.9 %copy-start.9 = (f32[1,256]{1,0:T(1,128)S(1)}, f32[1,256]{1,0:T(1,128)}, u32[]{:S(2)}) copy-start(f32[1,256]{1,0:T(1,128)} %param.20) | copy-start | bytes 3076
  62.0 10.2 %all-to-all-start.2 = ((f32[8,1,512]{2,1,0:T(1,128)}), f32[8,1,512]{2,1,0:T(1,128)S(1)}, u32[]{:S(2)}, u32[]{:S(2)}) async-start(f32[8,1,512]{2,1,0:T(1,128)} %reshape.119), calls=%async_computation.2 | async-start | bytes 32768 | tf_op jit(solution)/shard_map/all_to_all | solution.py:20
  98.0 18.0 %all-to-all-start.4 = ((f32[64,1,1]{2,1,0:T(1,128)}), f32[64,1,1]{2,1,0:T(1,128)S(1)}, u32[]{:S(2)}, u32[]{:S(2)}) async-start(f32[64,1,1]{2,1,0:T(1,128)} %broadcast_in_dim.72), calls=%async_computation.4 | async-start | bytes 65536 | tf_op jit(solution)/shard_map/all_to_all | solution.py:20
where the time goes:
time: 120 us; the launch traced here: 119 us
  blocking collectives  34.9 us (29%)
  waiting for transfers between devices  21.6 us (18%)
  starting transfers between devices  20.2 us (17%)
  local copies, waits for them, and re-layouts  17.8 us (15%)
  other arithmetic  12.1 us (10%)
  between operations  6.11 us (5%)
  matrix products  5.08 us (4%)
  loops' own time  1.38 us (1%)
    all_to_all x2, blocking collectives, from_everyone(): lax.all_to_all(jnp.broadcast_to(x[None], (devices, *x.shape)), axis, 0, 0...  34.9 us
    all_to_all x3, waiting for transfers between devices, from_everyone(): lax.all_to_all(jnp.broadcast_to(x[None], (devices, *x.shape)), axis, 0, 0...  21.6 us
    all_to_all x3, starting transfers between devices, from_everyone(): lax.all_to_all(jnp.broadcast_to(x[None], (devices, *x.shape)), axis, 0, 0...  20.2 us
    another operation x1, local copies, waits for them, and re-layouts, shards(): jnp.stack([offset_own, slope_own, jnp.sum(weight, axis=1), jnp.sum(weight...  5.2 us
    dynamic_update_slice x128, local copies, waits for them, and re-layouts, shards(): lax.scan(fold_step, start_pair, (table[:, :, 0], table[:, :, 1]), reverse...  4.78 us
    dot_general x1, matrix products, shards(): jnp.einsum('sth,h->st', hidden, scaled, precision=HIGHEST, preferred_elem...  3.34 us
    dot_general x1, other arithmetic, shards(): jnp.einsum('sth,sth->st', hidden, hidden, preferred_element_type=jnp.floa...  3.22 us
    broadcast_in_dim x5, local copies, waits for them, and re-layouts, from_everyone(): jnp.broadcast_to(x[None], (devices, *x.shape))  2.74 us
  transfers between devices with their start and end apart: 3, of which 3 were waited for; matrix products, arithmetic and copies ran while one was open for 1% of the time, Pallas kernels for 0%

commit v1 on v0

v1 whole, which is shorter than its diff:
```python
from functools import partial

import jax
import jax.numpy as jnp
from jax import lax
from jax.experimental import pallas as pl
from jax.experimental.pallas import tpu as pltpu
from jax.sharding import PartitionSpec as P

EPS_NORM = 1e-06
EPS_WHITE = 1e-08
CLIP = 0.2
LANES = 128
SUBS = 8
EXTRA = 16
F32 = jnp.float32
MESH = pl.DeviceIdType.MESH


def chip_grid(seq_count):
    return {64: (4, 16), 16: (4, 4), 4: (2, 2)}[seq_count]


def offsets_by_distance(nx, ny):
    def far(o):
        return min(o[0], nx - o[0]) + min(o[1], ny - o[1])

    every = [(dx, dy, dc) for dx in range(nx) for dy in range(ny) for dc in range(2)]
    return sorted(every[1:], key=lambda o: (-far(o), -o[2]))


def shift_lanes(x, count, fill, lane, width):
    moved = pltpu.roll(x, width - count, 1)
    return jnp.where(lane >= width - count, fill, moved)


def shift_rows(x, count, fill, row, height):
    moved = pltpu.roll(x, height - count, 0)
    return jnp.where(row >= height - count, fill, moved)


def picked(table, index):
    return jnp.take_along_axis(table, jnp.full(table.shape, index, jnp.int32), axis=1)


def kernel(
    sizes,
    hid, gain, wgt, rew, done, mask, newp, oldp, disc, trace, boot,
    out_v, out_w, out_l, out_s,
    buf, gain_v, wgt_v, rew_v, done_v, mask_v, new_v, old_v, disc_s, trace_s, boot_s,
    send_a, recv_a, mess_b, recv_b, mess_c, recv_c, mess_d, recv_d, mess_e, recv_e,
    res_v, res_w, res_l, res_s,
    hid_sem, in_sem, send_sem, recv_sem, out_sem,
):
    nx, nz, ny, length, features, total_features = sizes
    rows = 2 * ny
    seq = lax.axis_index("seq")
    t = lax.axis_index("tensor")
    x, z = lax.div(seq, nz), lax.rem(seq, nz)
    y, core = lax.div(t, 2), lax.rem(t, 2)

    def plane_peer(o):
        px = lax.rem(x + o[0], nx)
        py = lax.rem(y + o[1], ny)
        pc = core if o[2] == 0 else 1 - core
        return px, py * 2 + pc

    def ring_peer(d):
        return {"seq": x * nz + lax.rem(z + d, nz), "tensor": t}

    plane = offsets_by_distance(nx, ny)
    column = [o for o in plane if o[0] == 0] + [(0, 0, 0)]
    ring = sorted(range(1, nz), key=lambda d: -min(d, nz - d))

    order = [plane_peer(o)[1] for o in column]
    loads = [
        pltpu.make_async_copy(hid.at[order[k]], buf.at[k, pl.ds(0, length)], hid_sem.at[k])
        for k in range(rows)
    ]
    small = [
        (gain, gain_v), (wgt, wgt_v), (rew, rew_v), (done, done_v), (mask, mask_v),
        (newp, new_v), (oldp, old_v), (disc, disc_s), (trace, trace_s), (boot, boot_s),
    ]
    small = [pltpu.make_async_copy(a, b, in_sem.at[i]) for i, (a, b) in enumerate(small)]
    for c in small[:2]:
        c.start()
    for c in loads:
        c.start()
    for c in small[2:]:
        c.start()

    barrier = pltpu.get_barrier_semaphore()
    for d in ring:
        pl.semaphore_signal(barrier, inc=1, device_id=ring_peer(d), device_id_type=MESH)
    for o in plane:
        px, pt = plane_peer(o)
        pl.semaphore_signal(
            barrier, inc=1, device_id={"seq": px * nz + z, "tensor": pt}, device_id_type=MESH
        )

    for c in small[:2]:
        c.wait()
    scaled = gain_v[...].astype(F32) * wgt_v[...].astype(F32)
    high = scaled.astype(jnp.bfloat16).astype(F32)
    low = scaled - high
    extra_row = lax.broadcasted_iota(jnp.int32, (EXTRA, features), 0)
    both = jnp.where(
        extra_row == 0,
        jnp.broadcast_to(high.reshape(1, features), (EXTRA, features)),
        jnp.where(extra_row == 1, jnp.broadcast_to(low.reshape(1, features), (EXTRA, features)), 0.0),
    ).astype(jnp.bfloat16)
    for k in range(rows):
        buf[k, pl.ds(length, EXTRA)] = both

    eye = lax.broadcasted_iota(jnp.int32, (length, length), 0) == lax.broadcasted_iota(
        jnp.int32, (length, length), 1
    )
    for k in range(rows):
        loads[k].wait()
        gram = lax.dot_general(
            buf[k], buf[k, pl.ds(0, length)], (((1,), (1,)), ((), ())), preferred_element_type=F32
        )
        squares = jnp.sum(jnp.where(eye, gram[:length], 0.0), axis=0, keepdims=True)
        products = gram[length : length + 1] + gram[length + 1 : length + 2]
        if k < rows - 1:
            send_a[k, :, pl.ds(0, length)] = squares
            send_a[k, :, pl.ds(length, length)] = products
        else:
            recv_a[t, :, pl.ds(0, length)] = squares
            recv_a[t, :, pl.ds(length, length)] = products

    pl.semaphore_wait(barrier, nz - 1 + nx * rows - 1)

    def push(src, dst, stage, device):
        copy = pltpu.make_async_remote_copy(
            src_ref=src, dst_ref=dst, send_sem=send_sem.at[stage], recv_sem=recv_sem.at[stage],
            device_id=device, device_id_type=MESH,
        )
        copy.start()

    def arrived(slots, count, stage):
        part = slots.at[pl.ds(0, count)]
        pltpu.make_async_copy(part, part, recv_sem.at[stage]).wait()

    def left(slots, count, stage):
        part = slots.at[pl.ds(0, count)]
        pltpu.make_async_copy(part, part, send_sem.at[stage]).wait()

    def to_ring(mess, slots, stage):
        for d in ring:
            push(mess, slots.at[z], stage, ring_peer(d))

    def to_plane(mess, slots, stage):
        for o in plane:
            px, pt = plane_peer(o)
            push(mess, slots.at[x * rows + t], stage, {"seq": px * nz + z, "tensor": pt})

    for k in range(rows - 1):
        push(send_a.at[k], recv_a.at[t], 0, {"seq": seq, "tensor": order[k]})

    for c in small[2:]:
        c.wait()
    gamma, lam = disc_s[t], trace_s[t]
    wide = (SUBS, length)
    lane = lax.broadcasted_iota(jnp.int32, wide, 1)
    sub = lax.broadcasted_iota(jnp.int32, wide, 0)

    def spread(a):
        return jnp.broadcast_to(a, wide)

    rewards = spread(rew_v[pl.ds(t, 1)])
    alive = 1.0 - spread(done_v[pl.ds(t, 1)]).astype(F32)
    weight = spread(mask_v[...]).astype(F32)
    ratio = jnp.exp(spread(new_v[...]) - spread(old_v[...]))
    clipped = jnp.clip(ratio, 1.0 - CLIP, 1.0 + CLIP)
    last_pos = lane == length - 1
    reach = gamma * alive
    coef = jnp.where(last_pos, reach, (gamma * lam) * alive)
    coefs = []
    for step in range(length.bit_length() - 1):
        coefs.append(coef)
        coef = coef * shift_lanes(coef, 1 << step, 1.0, lane, length)
    ends = jnp.logical_and(x == nx - 1, z == nz - 1)
    known = jnp.where(ends, boot_s[t], 0.0)
    kept = jnp.where(ends, 0.0, 1.0)
    n_own = jnp.sum(weight, axis=1, keepdims=True)
    n_inv = 1.0 / jnp.maximum(n_own, 1.0)

    arrived(recv_a, rows - 1, 0)
    sums = jnp.sum(recv_a[...], axis=0)
    values = spread(sums[:, length:] * lax.rsqrt(sums[:, :length] / total_features + EPS_NORM))
    res_v[...] = values[:1]
    v_copy = pltpu.make_async_copy(res_v, out_v, out_sem.at[0])
    v_copy.start()

    local = rewards + reach * shift_lanes(values, 1, 0.0, lane, length) - values
    for step, c in enumerate(coefs):
        local = local + c * shift_lanes(local, 1 << step, 0.0, lane, length)
    local = local + coef * known
    coef = coef * kept
    mean_l = jnp.sum(weight * local, axis=1, keepdims=True) * n_inv
    mean_c = jnp.sum(weight * coef, axis=1, keepdims=True) * n_inv
    dev_l, dev_c = local - mean_l, coef - mean_c
    w_l, w_c = weight * dev_l, weight * dev_c
    table = jnp.zeros(wide, F32)
    first = lane == 0
    for i, q in enumerate(
        [jnp.where(first, values + lam * local, 0.0), jnp.where(first, lam * coef, 0.0),
         w_l * dev_l, w_l * dev_c, w_c * dev_c]
    ):
        table = jnp.where(sub == i, q, table)
    column_of = jnp.sum(table, axis=1, keepdims=True)
    sub1 = lax.broadcasted_iota(jnp.int32, (SUBS, 1), 0)
    for i, q in [(5, n_own), (6, mean_l), (7, mean_c)]:
        column_of = jnp.where(sub1 == i, q, column_of)
    tile = (SUBS, LANES)
    on_diagonal = lax.broadcasted_iota(jnp.int32, tile, 0) == lax.broadcasted_iota(jnp.int32, tile, 1)
    message = jnp.sum(
        jnp.where(on_diagonal, jnp.broadcast_to(column_of, tile), 0.0), axis=0, keepdims=True
    )
    mess_b[...] = message
    recv_b[z] = message
    to_ring(mess_b, recv_b, 1)

    arrived(recv_b, nz - 1, 1)
    got = recv_b[:, 0, :]
    row = lax.broadcasted_iota(jnp.int32, (nz, LANES), 0)
    zlane = lax.broadcasted_iota(jnp.int32, (nz, LANES), 1)
    o, s, m_ll, m_lc, m_cc, n, mu_l, mu_c = (picked(got, i) for i in range(8))
    run_o, run_s, step = o, s, 1
    while step < nz:
        run_o = run_o + run_s * shift_rows(run_o, step, 0.0, row, nz)
        run_s = run_s * shift_rows(run_s, step, 1.0, row, nz)
        step *= 2
    p = shift_rows(run_o, 1, 0.0, row, nz)
    q = shift_rows(run_s, 1, 1.0, row, nz)

    def down(a):
        return jnp.sum(a, axis=0, keepdims=True)

    a_blk, b_blk = mu_l + mu_c * p, mu_c * q
    n_line = down(n)
    n_line_inv = 1.0 / jnp.maximum(n_line, 1.0)
    a_line, b_line = down(n * a_blk) * n_line_inv, down(n * b_blk) * n_line_inv
    da, db = a_blk - a_line, b_blk - b_line
    m_aa = m_ll + 2.0 * p * m_lc + p * p * m_cc + n * da * da
    m_ab = q * m_lc + p * q * m_cc + n * da * db
    m_bb = q * q * m_cc + n * db * db
    line = jnp.where(zlane == 2, m_aa, jnp.where(zlane == 3, m_ab, jnp.where(zlane == 4, m_bb, 0.0)))
    line = jnp.where(
        row == 0, jnp.where(zlane == 0, run_o, jnp.where(zlane == 1, run_s, line)), line
    )
    message = down(line)
    lane1 = lax.broadcasted_iota(jnp.int32, (1, LANES), 1)
    for i, v in [(5, n_line), (6, a_line), (7, b_line)]:
        message = jnp.where(lane1 == i, v, message)
    mess_c[...] = message
    recv_c[x * rows + t] = message
    to_plane(mess_c, recv_c, 2)
    own_p = down(jnp.where(row == z, p, 0.0))
    own_q = down(jnp.where(row == z, q, 0.0))

    arrived(recv_c, nx * rows - 1, 2)
    got = recv_c[:, 0, :].reshape(nx, rows, LANES)
    rsub = lax.broadcasted_iota(jnp.int32, (rows, LANES), 0)
    entering = jnp.zeros((rows, LANES), F32)
    own_e = jnp.zeros((rows, LANES), F32)
    lines = []
    for i in reversed(range(nx)):
        o, s, m_aa, m_ab, m_bb, n, a, b = (picked(got[i], j) for j in range(8))
        own_e = jnp.where(jnp.logical_and(rsub == t, x == i), entering, own_e)
        lines.append(
            (n, a + b * entering, m_aa + 2.0 * entering * m_ab + entering * entering * m_bb)
        )
        entering = o + s * entering
    count = down(sum(n for n, _, _ in lines))
    mean = down(sum(n * mu for n, mu, _ in lines)) / count
    second = down(sum(m + n * (mu - mean) * (mu - mean) for n, mu, m in lines))
    scale = lax.rsqrt(second / count + EPS_WHITE)
    enter = own_p + own_q * down(own_e)

    def over(a):
        return jnp.broadcast_to(jnp.concatenate([a] * (length // LANES), axis=1), wide)

    white = (local + coef * over(enter) - over(mean)) * over(scale)
    loss = -weight * jnp.minimum(ratio * white, clipped * white)
    message = jnp.broadcast_to(jnp.sum(loss, axis=1, keepdims=True), tile)[:1]
    mess_d[...] = message
    recv_d[z] = message
    to_ring(mess_d, recv_d, 3)
    res_w[...] = white[:1]
    res_l[...] = loss[:1]
    w_copy = pltpu.make_async_copy(res_w, out_w, out_sem.at[1])
    w_copy.start()
    l_copy = pltpu.make_async_copy(res_l, out_l, out_sem.at[2])
    l_copy.start()

    arrived(recv_d, nz - 1, 3)
    message = down(recv_d[:, 0, :])
    mess_e[...] = message
    recv_e[x * rows + t] = message
    to_plane(mess_e, recv_e, 4)
    arrived(recv_e, nx * rows - 1, 4)
    res_s[...] = down(recv_e[:, 0, :]) / count
    s_copy = pltpu.make_async_copy(res_s, out_s, out_sem.at[3])
    s_copy.start()

    left(recv_a, rows - 1, 0)
    left(recv_b, nz - 1, 1)
    left(recv_c, nx * rows - 1, 2)
    left(recv_d, nz - 1, 3)
    left(recv_e, nx * rows - 1, 4)
    for c in (v_copy, w_copy, l_copy, s_copy):
        c.wait()


def shards(seq_count, total_features, *args):
    hidden = args[0]
    rows, length, features = hidden.shape
    nx, nz = chip_grid(seq_count)
    ny = rows // 2
    any_space = pl.BlockSpec(memory_space=pl.ANY)
    vmem, smem = pltpu.VMEM, pltpu.SMEM
    out = jax.ShapeDtypeStruct((1, length), F32)
    values, white, loss, total = pl.pallas_call(
        partial(kernel, (nx, nz, ny, length, features, total_features)),
        out_shape=[out, out, out, jax.ShapeDtypeStruct((1, LANES), F32)],
        in_specs=[any_space] * 11,
        out_specs=[any_space] * 4,
        scratch_shapes=[
            vmem((rows, length + EXTRA, features), jnp.bfloat16),
            vmem((features,), jnp.bfloat16),
            vmem((features,), jnp.bfloat16),
            vmem((rows, length), F32),
            vmem((rows, length), jnp.int32),
            vmem((1, length), jnp.int32),
            vmem((1, length), F32),
            vmem((1, length), F32),
            smem((rows,), F32),
            smem((rows,), F32),
            smem((rows,), F32),
            vmem((rows, 1, 2 * length), F32),
            vmem((rows, 1, 2 * length), F32),
            vmem((1, LANES), F32),
            vmem((nz, 1, LANES), F32),
            vmem((1, LANES), F32),
            vmem((nx * rows, 1, LANES), F32),
            vmem((1, LANES), F32),
            vmem((nz, 1, LANES), F32),
            vmem((1, LANES), F32),
            vmem((nx * rows, 1, LANES), F32),
            vmem((1, length), F32),
            vmem((1, length), F32),
            vmem((1, length), F32),
            vmem((1, LANES), F32),
            pltpu.SemaphoreType.DMA((rows,)),
            pltpu.SemaphoreType.DMA((10,)),
            pltpu.SemaphoreType.DMA((5,)),
            pltpu.SemaphoreType.DMA((5,)),
            pltpu.SemaphoreType.DMA((4,)),
        ],
        compiler_params=pltpu.CompilerParams(collective_id=0, has_side_effects=True),
        name="critic_gae",
    )(*args)
    return values, white, loss, total[0, 0]


def solution(mesh):
    seq_only = P(None, "seq")
    both = P("tensor", "seq")
    in_specs = (
        P(None, "seq", "tensor"), P("tensor"), P("tensor"), seq_only, seq_only,
        both, both, both, P(), P(), P(),
    )
    total_features = 1024 * mesh.shape["tensor"]
    return jax.shard_map(
        partial(shards, mesh.shape["seq"], total_features),
        mesh=mesh, in_specs=in_specs, out_specs=(both, both, both, P()), check_vma=False,
    )
```

time: 120 us -> 51.9 us (0.43)
  Pallas kernels: 0 us -> 45.7 us
  blocking collectives: 34.9 us -> 0 us
  waiting for transfers between devices: 21.6 us -> 0 us
  starting transfers between devices: 20.2 us -> 0 us
  local copies, waits for them, and re-layouts: 17.8 us -> 3.67 us
  other arithmetic: 12.1 us -> 0 us
  matrix products: 5.08 us -> 0 us
  between operations: 6.11 us -> 2.38 us
  loops' own time: 1.38 us -> 0 us
    pallas_call x0 -> x1, Pallas kernels: none -> 45.7 us  [shards(): pl.pallas_call(partial(kernel, (nx, nz, ny, length, features, total_featu...]
    all_to_all x2 -> x0, blocking collectives: 34.9 us -> none  [from_everyone(): lax.all_to_all(jnp.broadcast_to(x[None], (devices, *x.shape)), axis, 0, 0...]
    all_to_all x3 -> x0, waiting for transfers between devices: 21.6 us -> none  [from_everyone(): lax.all_to_all(jnp.broadcast_to(x[None], (devices, *x.shape)), axis, 0, 0...]
    all_to_all x3 -> x0, starting transfers between devices: 20.2 us -> none  [from_everyone(): lax.all_to_all(jnp.broadcast_to(x[None], (devices, *x.shape)), axis, 0, 0...]
    reduce_sum x7 -> x0, other arithmetic: 5.38 us -> none  [the longest x1 1.9 us: shards(): jnp.sum(token_loss)]
    another operation x5 -> x0, local copies, waits for them, and re-layouts: 5.21 us -> none  [the longest x1 5.2 us: shards(): jnp.stack([offset_own, slope_own, jnp.sum(weight, axis=1), jnp.sum(weight...]
    dot_general x2 -> x0, matrix products: 5.08 us -> none  [the longest x1 3.34 us: shards(): jnp.einsum('sth,h->st', hidden, scaled, precision=HIGHEST, preferred_elem...]
    dynamic_update_slice x128 -> x0, local copies, waits for them, and re-layouts: 4.78 us -> none  [shards(): lax.scan(fold_step, start_pair, (table[:, :, 0], table[:, :, 1]), reverse...]
  transfers between devices with their start and end apart: 3 -> 0, of which waited for: 3 -> 0; matrix products, arithmetic and copies ran while one was open for 1% -> 0% of each run, Pallas kernels for 0% -> 0%
where the time goes in v1:
time: 51.9 us; the launch traced here: 51.7 us
  Pallas kernels  45.7 us (88%)
  local copies, waits for them, and re-layouts  3.67 us (7%)
  between operations  2.38 us (5%)
    pallas_call x1, Pallas kernels, shards(): pl.pallas_call(partial(kernel, (nx, nz, ny, length, features, total_featu...  45.7 us
    unnamed x3, local copies, waits for them, and re-layouts  3.67 us

profile of v1, /device:TPU:1, one launch (start us, length us, event | category | flops | bytes accessed | tf_op | source)
XLA Modules:
  0.0 51.7 jit_solution(5845384949991326419)
XLA Ops:
  0.6 45.7 %critic_gae.1 = (f32[1,256]{1,0:T(1,128)}, f32[1,256]{1,0:T(1,128)}, f32[1,256]{1,0:T(1,128)}, f32[1,128]{1,0:T(1,128)}) custom-call(bf16[8,256,1024]{2,1,0:T(8,128)(2,1)} %hid.1, bf16[1024]{0:T(1024)(128)(2,1)} %gain.1, bf16[1024]{0:T(1024)(128)(2,1)} %wgt.1, f32[8,256]{1,0:T(8,128)} %rew.1, s32[8,256]{1,0:T(8,128)} %done.1, s32[1,256]{1,0:T(1,128)} %mask.1, ...), custom_call_target="tpu_custom_call" | custom-call | tf_op jit(solution)/shard_map/critic_gae/pallas_call | solution.py:325
  46.3 1.2 %copy.19 = f32[1,256]{1,0:T(1,128)} copy(f32[1,256]{1,0:T(1,128)} %get-tuple-element.16) | data formatting | bytes 2048
  47.5 1.2 %copy.20 = f32[1,256]{1,0:T(1,128)} copy(f32[1,256]{1,0:T(1,128)} %get-tuple-element.17) | data formatting | bytes 2048
  48.8 1.2 %copy.21 = f32[1,256]{1,0:T(1,128)} copy(f32[1,256]{1,0:T(1,128)} %get-tuple-element.18) | data formatting | bytes 2048
